TPU v7x, 32 devices: a whole 2x2x4 slice. The times are simulated.
32 devices in a mesh: batch: 8 (over z, x), head: 4 (over y, core).
Axes of the slice: x: 2, y: 2, z: 4, core: 2. Of those that a mesh axis runs over, the one named last changes fastest.
Arguments:
- tokens: bfloat16 [4096, 2048], P('batch', 'head'), may hold values from -96 to 96
- lengths: int32 [32], P('batch'), may hold values from 1 to 128
- states: float32 [32, 16, 128, 128], P('batch', 'head'), may hold values from -3 to 3
- norm_gain: float32 [2048], replicated, may hold values from 0.1 to 1.9
- mix_weight: bfloat16 [2048, 14336], P(None, 'head'), may hold values from -0.125 to 0.125
- rate_weight: bfloat16 [2048, 64], P(None, 'head'), may hold values from -0.5524272 to 0.5524272
- decay_rate: float32 [16], P('head'), may hold values from 0.0005 to 0.03
- head_gain: float32 [128], replicated, may hold values from 0.1 to 1.9
- out_weight: bfloat16 [2048, 2048], P('head'), may hold values from -0.125 to 0.125
- final_gain: float32 [2048], replicated, may hold values from 0.1 to 1.9
- vocab_table: bfloat16 [16384, 2048], P(('batch', 'head')), may hold values from -50.8233 to 50.8233
- next_token: int32 [32], replicated, may hold values from 0 to 16383
Outputs:
- mixed: bfloat16 [4096, 2048], P('batch', 'head')
- new_state: float32 [32, 16, 128, 128], P('batch', 'head')
- log_likelihood: float32 [32], replicated
All inputs are finite; a program needn't handle non-finite values.
Results may differ from a plain program's by a relative error of at most 0.0058.
The roundings to bfloat16 on the way count: a program that leaves them out, or rounds other values in their place, can miss the bound.
Values may be sent and summed in bfloat16 or wider, within the bound.
A program may use at most 128 MiB of HBM per device.

v0:
```python
import jax
import jax.numpy as jnp
from jax import lax
from jax.sharding import PartitionSpec as P

HEAD_DIM = 128
REFLECT = 3
NEW_POSITIONS = 128


ROW_EPSILON = 1e-05
KEY_EPSILON = 1e-06
HIGHEST_PRECISION = lax.Precision.HIGHEST


def joined(array, axis, combine):
    everything = jax.tree.map(lambda part: lax.all_gather(part, axis), array)
    initial = jax.tree.map(lambda part: part[0], everything)

    def step(k, so_far):
        return combine(so_far, jax.tree.map(lambda part: part[k], everything))

    return lax.fori_loop(1, lax.axis_size(axis), step, initial)


def delta_block(queries, key_rows, value_rows, beta_rows, log_decay, start_state):
    positions = key_rows.shape[0]
    reflections = key_rows.shape[1]
    total_steps = positions * reflections
    flat_keys = key_rows.reshape(total_steps, key_rows.shape[2])
    flat_values = value_rows.reshape(total_steps, value_rows.shape[2])
    flat_betas = beta_rows.reshape(total_steps)
    padding = jnp.zeros((positions, reflections - 1), log_decay.dtype)
    step_decay = jnp.concatenate([log_decay[:, None], padding], axis=1).reshape(total_steps)
    cumulative = jnp.cumsum(step_decay)
    step_index = jnp.arange(total_steps)
    earlier = step_index[:, None] > step_index[None, :]
    decay_ratio = jnp.exp(jnp.where(earlier, cumulative[:, None] - cumulative[None, :], -jnp.inf))
    key_gram = jnp.dot(flat_keys, flat_keys.T, precision=HIGHEST_PRECISION)
    system = (
        jnp.eye(total_steps, dtype=key_gram.dtype) + flat_betas[:, None] * decay_ratio * key_gram
    )
    start_image = jnp.dot(flat_keys, start_state.T, precision=HIGHEST_PRECISION)
    source = flat_betas[:, None] * (flat_values - jnp.exp(cumulative)[:, None] * start_image)
    updates = jax.scipy.linalg.solve_triangular(system, source, lower=True, unit_diagonal=True)
    query_cumulative = cumulative.reshape(positions, reflections)[:, reflections - 1]
    query_step = step_index.reshape(positions, reflections)[:, reflections - 1]
    visible = step_index[None, :] <= query_step[:, None]
    weights = jnp.exp(jnp.where(visible, query_cumulative[:, None] - cumulative[None, :], -jnp.inf))
    scores = jnp.dot(queries, flat_keys.T, precision=HIGHEST_PRECISION) * weights
    attended = jnp.exp(query_cumulative)[:, None] * jnp.dot(
        queries, start_state.T, precision=HIGHEST_PRECISION
    )
    attended = attended + jnp.dot(scores, updates, precision=HIGHEST_PRECISION)
    tail_decay = jnp.exp(cumulative[total_steps - 1] - cumulative)
    new_state = jnp.exp(cumulative[total_steps - 1]) * start_state
    new_state = new_state + jnp.dot(
        updates.T, tail_decay[:, None] * flat_keys, precision=HIGHEST_PRECISION
    )
    return (attended, new_state)


def head_inputs(projected, rate_logits, valid_mask, decay_rate):
    queries = jax.nn.silu(projected[:, :, :, 0])
    key_rows = jax.nn.silu(projected[:, :, :, 1 : REFLECT + 1])
    key_rows = key_rows * lax.rsqrt(
        jnp.sum(key_rows * key_rows, axis=-1, keepdims=True) + KEY_EPSILON
    )
    value_rows = jax.nn.silu(projected[:, :, :, REFLECT + 1 :])
    beta_rows = jnp.where(
        valid_mask[:, :, None, None], 2.0 * jax.nn.sigmoid(rate_logits[..., :REFLECT]), 0.0
    )
    log_decay = jnp.where(
        valid_mask[:, :, None], -decay_rate * jax.nn.softplus(rate_logits[..., REFLECT]), 0.0
    )
    return (queries, key_rows, value_rows, beta_rows, log_decay)


def run_heads(queries, key_rows, value_rows, beta_rows, log_decay, start_states):
    per_head = jax.vmap(delta_block, in_axes=(1, 1, 1, 1, 1, 0), out_axes=(1, 0))
    per_sequence = jax.vmap(per_head)
    return per_sequence(queries, key_rows, value_rows, beta_rows, log_decay, start_states)


def head_norm(attended, head_gain):
    factor = lax.rsqrt(jnp.mean(attended * attended, axis=-1, keepdims=True) + ROW_EPSILON)
    return (attended * factor * head_gain).astype(jnp.bfloat16)


def combine_totals(earlier_part, later_part):
    highest = jnp.maximum(earlier_part[0], later_part[0])
    summed = earlier_part[1] * jnp.exp(earlier_part[0] - highest) + later_part[1] * jnp.exp(
        later_part[0] - highest
    )
    return (highest, summed, earlier_part[2] + later_part[2])


def on_device(
    tokens,
    lengths,
    states,
    norm_gain,
    mix_weight,
    rate_weight,
    decay_rate,
    head_gain,
    out_weight,
    final_gain,
    vocab_table,
    next_token,
):
    sequences = lengths.shape[0]
    local_rows = tokens.shape[0]
    local_width = tokens.shape[1]
    model_width = norm_gain.shape[0]
    local_heads = states.shape[1]
    widened = tokens.astype(jnp.float32)
    row_squares = lax.psum(jnp.sum(widened * widened, axis=1), "head")
    initial = (
        jnp.zeros((local_rows, mix_weight.shape[1]), jnp.float32),
        jnp.zeros((local_rows, rate_weight.shape[1]), jnp.float32),
        jnp.zeros((local_rows,), jnp.float32),
    )
    wide_portion = lax.all_gather(tokens, "head", axis=1, tiled=True).astype(jnp.float32)
    scaled = (wide_portion * norm_gain).astype(jnp.bfloat16)
    projected = jnp.dot(scaled, mix_weight, preferred_element_type=jnp.float32)
    rate_logits = jnp.dot(scaled, rate_weight, preferred_element_type=jnp.float32)
    squares = initial[2]
    projected, rate_logits, squares = (projected, rate_logits, squares)
    inverse = lax.rsqrt(row_squares / model_width + ROW_EPSILON)
    projected = (projected * inverse[:, None]).reshape(
        sequences, NEW_POSITIONS, local_heads, 2 * REFLECT + 1, HEAD_DIM
    )
    rate_logits = (rate_logits * inverse[:, None]).reshape(
        sequences, NEW_POSITIONS, local_heads, REFLECT + 1
    )
    valid_mask = jnp.arange(NEW_POSITIONS)[None, :] < lengths[:, None]
    queries, key_rows, value_rows, beta_rows, log_decay = head_inputs(
        projected, rate_logits, valid_mask, decay_rate
    )
    attended, new_state = run_heads(queries, key_rows, value_rows, beta_rows, log_decay, states)
    normed = head_norm(attended, head_gain).reshape(local_rows, local_heads * HEAD_DIM)
    mix_sum = lax.psum_scatter(
        lax.dot_general(
            out_weight, normed, (((0,), (1,)), ((), ())), preferred_element_type=jnp.float32
        ),
        "head",
        scatter_dimension=0,
        tiled=True,
    ).T
    mixed = (tokens.astype(jnp.float32) + mix_sum).astype(jnp.bfloat16)
    last_index = (lengths - 1)[:, None, None]
    last_rows = jnp.take_along_axis(
        mixed.reshape(sequences, NEW_POSITIONS, local_width), last_index, axis=1
    )[:, 0]
    gathered = lax.all_gather(last_rows[None], ("batch", "head"), axis=0, tiled=True)
    batch_count = lax.axis_size("batch")
    head_count = lax.axis_size("head")
    everyone = gathered.reshape(batch_count, head_count, sequences, local_width).transpose(
        0, 2, 1, 3
    )
    everyone = everyone.reshape(batch_count * sequences, model_width)
    widened_all = everyone.astype(jnp.float32)
    factor = lax.rsqrt(jnp.mean(widened_all * widened_all, axis=1, keepdims=True) + ROW_EPSILON)
    hidden = (widened_all * factor * final_gain).astype(jnp.bfloat16)
    logits = jnp.dot(hidden, vocab_table.T, preferred_element_type=jnp.float32)
    vocab_here = vocab_table.shape[0]
    vocab_ids = lax.axis_index(("batch", "head")) * vocab_here + jnp.arange(vocab_here)
    largest = jnp.max(logits, axis=1)
    exp_total = jnp.sum(jnp.exp(logits - largest[:, None]), axis=1)
    target = jnp.sum(jnp.where(vocab_ids[None, :] == next_token[:, None], logits, 0.0), axis=1)
    largest, exp_total, target = joined(
        (largest, exp_total, target), ("batch", "head"), combine_totals
    )
    return (mixed, new_state, target - (largest + jnp.log(exp_total)))


def solution(mesh):
    placed = (
        P("batch", "head"),
        P("batch"),
        P("batch", "head", None, None),
        P(),
        P(None, "head"),
        P(None, "head"),
        P("head"),
        P(),
        P("head", None),
        P(),
        P(("batch", "head"), None),
        P(),
    )
    return jax.shard_map(
        on_device,
        mesh=mesh,
        in_specs=placed,
        out_specs=(P("batch", "head"), P("batch", "head", None, None), P()),
        check_vma=False,
    )
```

profile of v0, /device:TPU:0, one launch (start us, length us, event | category | flops | bytes accessed | tf_op | source)
XLA Modules:
  0.0 809.6 jit_solution(2534234138664865405)
XLA Ops:
  9.8 8.4 %psum.7 = f32[512]{0:T(512)S(1)} all-reduce(f32[512]{0:T(512)S(1)} %fusion.47), channel_id=1, replica_groups=mesh['batch'=8,'head'=4] {'head'}, use_global_device_ids=true, to_apply=%region_1.0 | all-reduce | flops 512 | bytes 4096 | tf_op jit(solution)/shard_map/psum | solution.py:118
  21.0 13.9 %all-gather.5.cloned.1.call-done = bf16[512,2048]{1,0:T(8,128)(2,1)} async-done(((bf16[512,512]{1,0:T(8,128)(2,1)}), bf16[512,2048]{1,0:T(8,128)(2,1)}) %all-gather.5.cloned.1.call-update) | async-done | bytes 2097168 | tf_op jit(solution)/shard_map/all_gather | solution.py:124
  40.5 4.8 reduce-window.6
  47.7 13.5 %convolution_multiply_fusion = f32[512,3584]{1,0:T(8,128)} fusion(bf16[2048,3584]{1,0:T(8,128)(2,1)} %param.18, f32[512]{0:T(512)S(1)} %add_rsqrt_fusion.3, bf16[512,2048]{1,0:T(8,128)(2,1)} %all-gather.5.cloned.1.call-done, f32[2048]{0:T(1024)S(1)} %copy-done.22), kind=kOutput, calls=%fused_computation.14 | convolution fusion | flops 7521173504 | bytes 24127488 | tf_op jit(solution)/shard_map/dot_general | solution.py:126
  61.2 10.5 %reshape.303 = f32[4,128,4,7,128]{4,3,2,1,0:T(8,128)} reshape(f32[512,3584]{1,0:T(8,128)} %convolution_multiply_fusion) | data formatting | bytes 14680064 | tf_op jit(solution)/shard_map/reshape | solution.py:131
  71.7 4.4 slice.101
  76.1 11.6 %fusion.74 = (f32[4,128,4,3,128]{4,3,2,1,0:T(4,128)}, f32[4,128,4,3,128]{4,3,2,1,0:T(4,128)}) fusion(f32[4,128,4,7,128]{4,3,2,1,0:T(8,128)} %reshape.303), kind=kLoop, calls=%fused_computation.124 | loop fusion | bytes 12582912 | tf_op jit(solution)/shard_map/slice | solution.py:65
  96.3 4.9 copy.142
  107.5 5.0 copy.109
  112.4 4.9 copy.144
  117.3 5.2 fusion.10
  122.5 4.9 copy.115
  127.4 7.3 fusion.19
  134.7 14.4 %select_add_fusion = f32[4,4,384,384]{3,2,1,0:T(8,128)} fusion(f32[384,384]{1,0:T(8,128)S(1)} %copy-done.15, f32[4,4,384]{2,1,0:T(4,128)S(1)} %reduce_window_sum.35, f32[4,4,384]{2,1,0:T(4,128)S(1)} %mul.212, f32[384,384]{1,0:T(8,128)S(1)} %copy-done.14, pred[384,384]{1,0:T(8,128)(4,1)S(1)} %get-tuple-element.236, ...), kind=kOutput, calls=%fused_computation.13 | convolution fusion | flops 3640393728 | bytes 14106624 | tf_op jit(solution)/shard_map/vmap(vmap())/dot_general | solution.py:39
  149.1 14.4 %while.21 = (s32[]{:T(128)}, f32[4,4,384,384]{3,2,1,0:T(8,128)}, s32[3,2]{0,1:T(2,128)S(1)}, f32[3,4,4,128,128]{4,3,0,2,1:T(8,128)}, s32[]{:T(128)}) while((s32[]{:T(128)}, f32[4,4,384,384]{3,2,1,0:T(8,128)}, s32[3,2]{0,1:T(2,128)S(1)}, f32[3,4,4,128,128]{4,3,0,2,1:T(8,128)}, s32[]{:T(128)}) %tuple.67), condition=%wide.while_cond, body=%wide.while_body.sunk | while | flops 2 | bytes 2098285 | solution.py:45
  154.7 4.3 bitcast_dynamic-update-slice_fusion.2
  163.5 473.1 %custom-call.4 = f32[4,4,3,128,128]{3,4,2,1,0:T(8,128)} custom-call(f32[4,4,3,128,128]{4,3,2,1,0:T(8,128)} %bitcast.131), custom_call_target="InvertDiagBlocksLowerTriangular" | custom-call | tf_op jit(solution)/shard_map/vmap(vmap(jit(_solve_triangular)))/triangular_solve | solution.py:45
  636.6 6.0 fusion.9
  648.9 4.5 fusion.33
  655.5 6.2 fusion.38
  677.8 6.6 fusion.43
  684.4 31.8 %reduce-scatter.2.cloned.1.call-done = f32[512,512]{0,1:T(8,128)} async-done(((f32[2048,512]{0,1:T(8,128)}), f32[512,512]{0,1:T(8,128)}) %reduce-scatter.2.cloned.1.call-update) | async-done | bytes 1048592 | tf_op jit(solution)/shard_map/reduce_scatter | solution.py:143
  718.5 40.8 %all_gather.25 = bf16[32,4,512]{2,1,0:T(4,128)(2,1)S(1)} all-gather(bf16[1,4,512]{2,1,0:T(4,128)(2,1)S(1)} %bitcast_select_fusion), channel_id=1, replica_groups=mesh['batch'=8,'head'=4] {'batch','head'}, dimensions={0}, use_global_device_ids=true | all-gather | bytes 135168 | tf_op jit(solution)/shard_map/all_gather | solution.py:156
  763.1 37.0 %all-reduce.4 = (f32[1024]{0:T(1024)S(1)}, f32[1024]{0:T(1024)S(1)}, f32[1024]{0:T(1024)S(1)}) all-reduce(f32[1024]{0:T(1024)S(1)} %dynamic-update-slice.2, f32[1024]{0:T(1024)S(1)} %dynamic-update-slice.3, f32[1024]{0:T(1024)S(1)} %dynamic-update-slice.4), channel_id=2, replica_groups=mesh['batch'=8,'head'=4] {'batch','head'}, use_global_device_ids=true, to_apply=%add.1 | all-reduce | flops 3072 | bytes 24576
  (173 shorter events, 71.5 us)
Async XLA Ops:
  7.2 660.2 %copy-start = (bf16[512,2048]{1,0:T(8,128)(2,1)S(1)}, bf16[512,2048]{1,0:T(8,128)(2,1)}, u32[]{:S(2)}) copy-start(bf16[512,2048]{1,0:T(8,128)(2,1)} %param.22) | copy-start | bytes 6291460
  7.2 27.7 %all-gather.5.cloned.1.call-start = ((), (), s32[]{:S(2)}) async-start(), calls=%async_computation.1 | async-start | bytes 2621440 | tf_op jit(solution)/shard_map/all_gather | solution.py:124
  7.9 708.3 %reduce-scatter.2.cloned.1.call-start = ((), (), s32[]{:S(2)}) async-start(), calls=%async_computation.2 | async-start | bytes 5242880 | tf_op jit(solution)/shard_map/reduce_scatter | solution.py:143
  37.1 10.6 %copy-start.22 = (f32[2048]{0:T(1024)S(1)}, f32[2048]{0:T(1024)}, u32[]{:S(2)}) copy-start(f32[2048]{0:T(1024)} %param.17) | copy-start | bytes 24580
  37.2 24.1 %copy-start.16 = (f32[4,128,4,4]{1,0,3,2:T(4,128)}, f32[4,128,4,4]{1,0,3,2:T(4,128)S(1)}, u32[]{:S(2)}) copy-start(f32[4,128,4,4]{1,0,3,2:T(4,128)S(1)} %reshape.243) | copy-start | bytes 98308
  76.1 51.2 %copy-start.9 = (f32[4,128,4,1,128]{4,3,2,1,0:T(1,128)}, f32[4,128,4,1,128]{4,3,2,1,0:T(1,128)S(1)}, u32[]{:S(2)}) copy-start(f32[4,128,4,1,128]{4,3,2,1,0:T(1,128)S(1)} %slice.101) | copy-start | bytes 3145732
  76.1 11.6 %slice-start = ((f32[4,128,4,4]{1,0,3,2:T(4,128)}), f32[4,128,4,3]{1,0,3,2:T(4,128)S(1)}, s32[]{:S(2)}) async-start(f32[4,128,4,4]{1,0,3,2:T(4,128)} %copy-done.16), calls=%async_computation.3 | async-start | bytes 49152 | tf_op jit(solution)/shard_map/slice | solution.py:71
  127.4 7.4 copy-start.1
  127.4 7.4 copy-start.14
  127.4 7.4 copy-start.15
  149.1 487.5 %copy-start.4 = (f32[4,4,128,128]{3,2,1,0:T(8,128)S(1)}, f32[4,4,128,128]{3,2,1,0:T(8,128)}, u32[]{:S(2)}) copy-start(f32[4,4,128,128]{3,2,1,0:T(8,128)} %param.16) | copy-start | bytes 3145732
  636.6 6.0 copy-start.12
  648.9 6.5 copy-start.2
  648.9 6.5 copy-start.17
  648.9 6.5 copy-start.19
  655.4 6.3 copy-start.7
  655.5 6.3 copy-start.5
  655.5 6.3 copy-start.10
  673.6 4.2 copy-start.3
  673.6 4.2 copy-start.6
  673.6 4.2 copy-start.8
  684.4 75.3 %copy-start.18 = (f32[2048]{0:T(1024)S(1)}, f32[2048]{0:T(1024)}, u32[]{:S(2)}) copy-start(f32[2048]{0:T(1024)} %param.23) | copy-start | bytes 24580
  684.4 78.0 %copy-start.21 = (s32[32]{0:T(128)S(1)}, s32[32]{0:T(128)}, u32[]{:S(2)}) copy-start(s32[32]{0:T(128)} %param.25) | copy-start | bytes 388
  717.8 84.5 %copy-start.13 = (bf16[512,512]{1,0:T(8,128)(2,1)}, bf16[512,512]{1,0:T(8,128)(2,1)S(1)}, u32[]{:S(2)}) copy-start(bf16[512,512]{1,0:T(8,128)(2,1)S(1)} %fusion.48) | copy-start | bytes 1572868
  (3 other events, 5.2 us)
Sparse Core Ops, SparseCore 0:
  9.5 25.2 all-gather.4
  671.8 44.3 reduce-scatter.1
where the time goes:
time: 820 us; the launch traced here: 810 us
  other arithmetic  505 us (62%)
  blocking collectives  86.2 us (11%)
  matrix products  78.2 us (10%)
  local copies, waits for them, and re-layouts  77.8 us (9%)
  waiting for transfers between devices  46.4 us (6%)
  between operations  15 us (2%)
    another operation x3, other arithmetic, delta_block(): jax.scipy.linalg.solve_triangular(system, source, lower=True, unit_diagon...  473 us
    all_gather x1, blocking collectives, on_device(): lax.all_gather(last_rows[None], ('batch', 'head'), axis=0, tiled=True)  40.8 us
    unnamed x1, blocking collectives  37 us
    reduce_scatter x1, waiting for transfers between devices, on_device(): lax.psum_scatter(lax.dot_general(out_weight, normed, (((0,), (1,)), ((),...  31.8 us
    another operation x16, local copies, waits for them, and re-layouts  18.4 us
  transfers between devices with their start and end apart: 2, of which 2 were waited for; matrix products, arithmetic and copies ran while one was open for 2% of the time, Pallas kernels for 0%

commit v1 on v0

v1 whole, which is shorter than its diff:
```python
import functools
import jax
import jax.numpy as jnp
from jax import lax
from jax.experimental import pallas as pl
from jax.experimental.pallas import tpu as pltpu
from jax.sharding import PartitionSpec as P

HEAD_DIM = 128
REFLECT = 3
NEW_POSITIONS = 128
STEPS = NEW_POSITIONS * REFLECT
BLOCK = 128

ROW_EPSILON = 1e-05
KEY_EPSILON = 1e-06
MESH = pl.DeviceIdType.MESH
F32 = jnp.float32
BF16 = jnp.bfloat16


def halves(x):
    high = x.astype(BF16)
    low = (x - high.astype(F32)).astype(BF16)
    return high, low


def left_side(x):
    return jnp.concatenate(halves(x), axis=1)


def right_side(x):
    row = jnp.concatenate(halves(x), axis=1)
    return jnp.concatenate([row, row], axis=0)


def right_transposed(x):
    high, low = halves(x)
    return jnp.concatenate(
        [jnp.concatenate([high, high], axis=1), jnp.concatenate([low, low], axis=1)], axis=0
    )


def folded(both):
    width = both.shape[1] // 2
    return both[:, :width] + both[:, width:]


def mm(left, right):
    return folded(jnp.dot(left, right, preferred_element_type=F32))


def mm_t(left, right):
    return folded(
        lax.dot_general(left, right, (((1,), (1,)), ((), ())), preferred_element_type=F32)
    )


def silu(x):
    return x / (1.0 + jnp.exp(-x))


def mixer_kernel(
    heads,
    lengths_ref,
    decay_ref,
    proj_ref,
    inverse_ref,
    rates_ref,
    gain_ref,
    state_ref,
    normed_ref,
    new_state_ref,
    keys_ref,
    scaled_keys_ref,
    scaled_values_ref,
):
    sequence = pl.program_id(0)
    group = pl.program_id(1)
    length = lengths_ref[sequence]
    inverse = inverse_ref[...]
    position = lax.broadcasted_iota(jnp.int32, (NEW_POSITIONS, 1), 0)
    valid = position < length
    rates = rates_ref[0] * inverse
    blocks = STEPS // BLOCK
    row_id = lax.broadcasted_iota(jnp.int32, (BLOCK, BLOCK), 0)
    col_id = lax.broadcasted_iota(jnp.int32, (BLOCK, BLOCK), 1)
    step_row = lax.broadcasted_iota(jnp.int32, (STEPS, NEW_POSITIONS), 0)
    step_col = lax.broadcasted_iota(jnp.int32, (STEPS, NEW_POSITIONS), 1)
    summing = jnp.concatenate(
        [
            jnp.where(step_col * REFLECT <= step_row, 1.0, 0.0).astype(F32),
            jnp.where(col_id <= row_id, 1.0, 0.0).astype(F32),
        ],
        axis=0,
    )
    queries, decays = [], []
    for i in range(heads):
        base = i * (2 * REFLECT + 1) * HEAD_DIM

        def part(k):
            start = base + k * HEAD_DIM
            return silu(proj_ref[:, start : start + HEAD_DIM] * inverse)

        queries.append(part(0))
        for j in range(REFLECT):
            rate = i * (REFLECT + 1)
            beta = jnp.where(
                valid, 2.0 / (1.0 + jnp.exp(-rates[:, rate + j : rate + j + 1])), 0.0
            )
            key = part(1 + j)
            key = key * lax.rsqrt(jnp.sum(key * key, axis=1, keepdims=True) + KEY_EPSILON)
            places = pl.ds(j, NEW_POSITIONS, REFLECT)
            keys_ref.at[i][places, :] = key
            scaled_keys_ref.at[i][places, :] = key * beta
            scaled_values_ref.at[i][places, :] = part(1 + REFLECT + j) * beta
        logit = rates[:, i * (REFLECT + 1) + REFLECT : (i + 1) * (REFLECT + 1)]
        softplus = jnp.maximum(logit, 0.0) + jnp.log1p(jnp.exp(-jnp.abs(logit)))
        rate_here = decay_ref[group * heads + i]
        log_decay = jnp.where(valid, -rate_here * softplus, 0.0)
        decays.append(
            jnp.dot(
                summing,
                jnp.broadcast_to(log_decay, (NEW_POSITIONS, HEAD_DIM)),
                preferred_element_type=F32,
                precision=lax.Precision.HIGHEST,
            )
        )

    def rows(x, b):
        return x[b * BLOCK : (b + 1) * BLOCK]

    lower, inverses, scores, sources, carried, tails, flipped = {}, {}, {}, {}, [], [], {}
    for i in range(heads):
        decay_column = decays[i]
        query_decay = decay_column[STEPS:]
        left_scaled = left_side(scaled_keys_ref[i])
        left_query = left_side(queries[i])
        start = right_transposed(state_ref[0, i])
        image = mm_t(left_scaled, start)
        grown = jnp.exp(decay_column[:STEPS])
        source = scaled_values_ref[i] - grown * image
        carried.append(jnp.exp(query_decay) * mm_t(left_query, start))
        last = query_decay[NEW_POSITIONS - 1 :]
        tail = jnp.exp(last - decay_column[:STEPS])
        tails.append((jnp.exp(last), tail * keys_ref[i]))
        for b in range(blocks):
            sources[i, b] = rows(source, b)
            flip = rows(decay_column, b).T
            right = right_transposed(keys_ref[i, b * BLOCK : (b + 1) * BLOCK, :])
            for a in range(b, blocks):
                gram = mm_t(rows(left_scaled, a), right)
                ratio = jnp.exp(jnp.minimum(rows(decay_column, a) - flip, 0.0))
                value = gram * ratio
                if a == b:
                    value = jnp.where(row_id > col_id, value, 0.0)
                lower[i, a, b] = value
            seen = b * BLOCK + col_id < (row_id + 1) * REFLECT
            weight = jnp.exp(jnp.minimum(query_decay - flip, 0.0))
            scores[i, b] = jnp.where(seen, mm_t(left_query, right) * weight, 0.0)

    chains = [(i, b) for i in range(heads) for b in range(blocks)]
    differ = row_id ^ col_id
    identity = jnp.where(row_id == col_id, 1.0, 0.0).astype(F32)
    for chain in chains:
        i, b = chain
        inverses[chain] = identity - jnp.where(differ == 1, lower[i, b, b], 0.0)
    level = 1
    while (1 << level) < BLOCK:
        crossing = (differ >> level) == 1
        for chain in chains:
            i, b = chain
            x = inverses[chain]
            border = right_side(jnp.where(crossing, lower[i, b, b], 0.0))
            first = mm(left_side(x), border)
            inverses[chain] = x - mm(left_side(first), right_side(x))
        level += 1

    updates = {}
    for b in range(blocks):
        for i in range(heads):
            source = sources[i, b]
            for a in range(b):
                source = source - mm(left_side(lower[i, b, a]), updates[i, a])
            update = mm(left_side(inverses[i, b]), right_side(source))
            updates[i, b] = right_side(update)
            grown, _ = tails[i]
            carried[i] = carried[i] + mm(left_side(scores[i, b]), updates[i, b])
            sources[i, b] = update
    for i in range(heads):
        factor = lax.rsqrt(
            jnp.mean(carried[i] * carried[i], axis=1, keepdims=True) + ROW_EPSILON
        )
        normed_ref[:, i * HEAD_DIM : (i + 1) * HEAD_DIM] = (
            carried[i] * factor * gain_ref[...]
        ).astype(BF16)
        grown, tail = tails[i]
        total = grown * state_ref[0, i]
        for b in range(blocks):
            total = total + mm(left_side(sources[i, b].T), right_side(rows(tail, b)))
        new_state_ref[0, i] = total


def mixer(projected, inverse, rate_logits, lengths, decay_rate, head_gain, states):
    sequences, local_heads = states.shape[0], states.shape[1]
    heads = 2 if local_heads % 2 == 0 else 1
    groups = local_heads // heads
    local_rows = projected.shape[0]
    per_head = REFLECT + 1
    rates = rate_logits.reshape(local_rows, groups, heads * per_head).transpose(1, 0, 2)
    wide = heads * (2 * REFLECT + 1) * HEAD_DIM
    smem = pl.BlockSpec(memory_space=pltpu.SMEM)
    state_spec = pl.BlockSpec((1, heads, HEAD_DIM, HEAD_DIM), lambda s, g: (s, g, 0, 0))
    steps = pltpu.VMEM((heads, STEPS, HEAD_DIM), F32)
    return pl.pallas_call(
        functools.partial(mixer_kernel, heads),
        grid=(sequences, groups),
        in_specs=[
            smem,
            smem,
            pl.BlockSpec((NEW_POSITIONS, wide), lambda s, g: (s, g)),
            pl.BlockSpec((NEW_POSITIONS, 1), lambda s, g: (s, 0)),
            pl.BlockSpec((1, NEW_POSITIONS, heads * per_head), lambda s, g: (g, s, 0)),
            pl.BlockSpec((1, HEAD_DIM), lambda s, g: (0, 0)),
            state_spec,
        ],
        out_specs=[
            pl.BlockSpec((NEW_POSITIONS, heads * HEAD_DIM), lambda s, g: (s, g)),
            state_spec,
        ],
        out_shape=[
            jax.ShapeDtypeStruct((local_rows, local_heads * HEAD_DIM), BF16),
            jax.ShapeDtypeStruct(states.shape, F32),
        ],
        scratch_shapes=[steps, steps, steps],
        name="mixer",
    )(lengths, decay_rate, projected, inverse, rates, head_gain[None], states)


def tail_kernel(
    batch_count,
    head_count,
    last_ref,
    gain_ref,
    table_hbm,
    next_ref,
    out_ref,
    table_ref,
    rows_ref,
    wide_ref,
    own_ref,
    stats_ref,
    table_sem,
    row_send,
    row_recv,
    stat_send,
    stat_recv,
):
    count = batch_count * head_count
    batch_at, head_at = lax.axis_index("batch"), lax.axis_index("head")
    me = batch_at * head_count + head_at
    sequences, width = last_ref.shape
    vocab_here = table_ref.shape[0]

    load = pltpu.make_async_copy(table_hbm, table_ref, table_sem)
    load.start()

    def other(k):
        index = lax.rem(me + k, count)
        return index, {"batch": index // head_count, "head": lax.rem(index, head_count)}

    barrier = pltpu.get_barrier_semaphore()

    @pl.loop(1, count)
    def _(k):
        pl.semaphore_signal(barrier, inc=1, device_id=other(k)[1], device_id_type=MESH)

    pl.semaphore_wait(barrier, count - 1)

    def row_copy(k, slot):
        return pltpu.make_async_remote_copy(
            src_ref=last_ref,
            dst_ref=rows_ref.at[slot],
            send_sem=row_send.at[k],
            recv_sem=row_recv.at[slot],
            device_id=other(k)[1],
            device_id_type=MESH,
        )

    @pl.loop(1, count)
    def _(k):
        row_copy(k, me).start()

    rows_ref[me] = last_ref[...]

    @pl.loop(1, count)
    def _(k):
        row_copy(k, other(k)[0]).wait_recv()

    for b in range(batch_count):
        for h in range(head_count):
            wide_ref[b * sequences : (b + 1) * sequences, h * width : (h + 1) * width] = rows_ref[
                b * head_count + h
            ].astype(F32)
    everyone = wide_ref[...]
    factor = lax.rsqrt(jnp.mean(everyone * everyone, axis=1, keepdims=True) + ROW_EPSILON)
    hidden = (everyone * factor * gain_ref[...]).astype(BF16)
    load.wait()
    logits = lax.dot_general(
        table_ref[...], hidden, (((1,), (1,)), ((), ())), preferred_element_type=F32
    )
    ids = lax.broadcasted_iota(jnp.int32, logits.shape, 0) + me * vocab_here
    largest = jnp.max(logits, axis=0, keepdims=True)
    own_ref[0:1, :] = largest
    own_ref[1:2, :] = jnp.sum(jnp.exp(logits - largest), axis=0, keepdims=True)
    own_ref[2:3, :] = jnp.sum(
        jnp.where(ids == next_ref[...], logits, 0.0), axis=0, keepdims=True
    )
    own_ref[3:, :] = jnp.zeros((own_ref.shape[0] - 3, own_ref.shape[1]), F32)

    def stat_copy(k, slot):
        return pltpu.make_async_remote_copy(
            src_ref=own_ref,
            dst_ref=stats_ref.at[slot],
            send_sem=stat_send.at[k],
            recv_sem=stat_recv.at[slot],
            device_id=other(k)[1],
            device_id_type=MESH,
        )

    @pl.loop(1, count)
    def _(k):
        stat_copy(k, me).start()

    stats_ref[me] = own_ref[...]

    @pl.loop(1, count)
    def _(k):
        row_copy(k, me).wait_send()
        stat_copy(k, other(k)[0]).wait_recv()

    highest = lax.fori_loop(
        0, count, lambda d, top: jnp.maximum(top, stats_ref[d][0:1]), largest
    )

    def add(d, totals):
        entry = stats_ref[d]
        return (totals[0] + entry[1:2] * jnp.exp(entry[0:1] - highest), totals[1] + entry[2:3])

    zero = jnp.zeros_like(largest)
    summed, target = lax.fori_loop(0, count, add, (zero, zero))
    out_ref[...] = target - (highest + jnp.log(summed))

    @pl.loop(1, count)
    def _(k):
        stat_copy(k, me).wait_send()


def tail(last_rows, final_gain, vocab_table, next_token):
    batch_count, head_count = lax.axis_size("batch"), lax.axis_size("head")
    count = batch_count * head_count
    sequences, width = last_rows.shape
    everyone = next_token.shape[0]
    vmem = pl.BlockSpec(memory_space=pltpu.VMEM)
    semaphores = pltpu.SemaphoreType.DMA((count,))
    return pl.pallas_call(
        functools.partial(tail_kernel, batch_count, head_count),
        out_shape=jax.ShapeDtypeStruct((1, everyone), F32),
        in_specs=[vmem, vmem, pl.BlockSpec(memory_space=pl.ANY), vmem],
        out_specs=vmem,
        scratch_shapes=[
            pltpu.VMEM(vocab_table.shape, BF16),
            pltpu.VMEM((count, sequences, width), BF16),
            pltpu.VMEM((everyone, final_gain.shape[0]), F32),
            pltpu.VMEM((8, everyone), F32),
            pltpu.VMEM((count, 8, everyone), F32),
            pltpu.SemaphoreType.DMA,
            semaphores,
            semaphores,
            semaphores,
            semaphores,
        ],
        compiler_params=pltpu.CompilerParams(collective_id=1, has_side_effects=True),
        name="tail",
    )(last_rows, final_gain[None], vocab_table, next_token[None])[0]


def on_device(
    tokens,
    lengths,
    states,
    norm_gain,
    mix_weight,
    rate_weight,
    decay_rate,
    head_gain,
    out_weight,
    final_gain,
    vocab_table,
    next_token,
):
    sequences = lengths.shape[0]
    local_width = tokens.shape[1]
    model_width = norm_gain.shape[0]
    wide = lax.all_gather(tokens, "head", axis=1, tiled=True).astype(F32)
    scaled = (wide * norm_gain).astype(BF16)
    inverse = lax.rsqrt(jnp.sum(wide * wide, axis=1, keepdims=True) / model_width + ROW_EPSILON)
    projected = jnp.dot(scaled, mix_weight, preferred_element_type=F32)
    rate_logits = jnp.dot(scaled, rate_weight, preferred_element_type=F32)
    normed, new_state = mixer(
        projected, inverse, rate_logits, lengths, decay_rate, head_gain, states
    )
    mix_sum = lax.psum_scatter(
        lax.dot_general(
            out_weight, normed, (((0,), (1,)), ((), ())), preferred_element_type=F32
        ),
        "head",
        scatter_dimension=0,
        tiled=True,
    ).T
    mixed = (tokens.astype(F32) + mix_sum).astype(BF16)
    last_index = (lengths - 1)[:, None, None]
    last_rows = jnp.take_along_axis(
        mixed.reshape(sequences, NEW_POSITIONS, local_width), last_index, axis=1
    )[:, 0]
    log_likelihood = tail(last_rows, final_gain, vocab_table, next_token)
    return (mixed, new_state, log_likelihood)


def solution(mesh):
    placed = (
        P("batch", "head"),
        P("batch"),
        P("batch", "head", None, None),
        P(),
        P(None, "head"),
        P(None, "head"),
        P("head"),
        P(),
        P("head", None),
        P(),
        P(("batch", "head"), None),
        P(),
    )
    return jax.shard_map(
        on_device,
        mesh=mesh,
        in_specs=placed,
        out_specs=(P("batch", "head"), P("batch", "head", None, None), P()),
        check_vma=False,
    )
```

time: 820 us -> 174 us (0.21); the launches traced: 810 us -> 174 us
  other arithmetic: 505 us -> 4.17 us
  blocking collectives: 86.2 us -> 0 us
  local copies, waits for them, and re-layouts: 77.8 us -> 3.61 us
  Pallas kernels: 0 us -> 59.9 us
  matrix products: 78.2 us -> 20.1 us
  waiting for transfers between devices: 46.4 us -> 72.1 us
    another operation x6 -> x0, other arithmetic: 478 us -> none  [the longest x3 473 us: delta_block(): jax.scipy.linalg.solve_triangular(system, source, lower=True, unit_diagon...]
    pallas_call x0 -> x2, Pallas kernels: none -> 59.9 us  [the longest x1 41 us: mixer(): pl.pallas_call(functools.partial(mixer_kernel, heads), grid=(sequences, g...]
    dot_general x9 -> x2, matrix products: 61.3 us -> 15.7 us  [the longest x1 13.5 us: on_device(): projected = jnp.dot(scaled, mix_weight, preferred_element_type=F32)]
    all_gather x1 -> x0, blocking collectives: 40.8 us -> none  [on_device(): lax.all_gather(last_rows[None], ('batch', 'head'), axis=0, tiled=True)]
    unnamed x1 -> x0, blocking collectives: 37 us -> none
    another operation x17 -> x0, local copies, waits for them, and re-layouts: 18.4 us -> none
    slice x9 -> x0, local copies, waits for them, and re-layouts: 16.2 us -> none  [the longest x1 11.6 us: head_inputs(): key_rows = jax.nn.silu(projected[:, :, :, 1:REFLECT + 1])]
    all_gather x1, waiting for transfers between devices: 13.9 us -> 26.9 us  [on_device(): wide = lax.all_gather(tokens, 'head', axis=1, tiled=True).astype(F32)]
  transfers between devices with their start and end apart: 2 -> 2, of which waited for: 2 -> 2; matrix products, arithmetic and copies ran while one was open for 2% -> 0% of each run, Pallas kernels for 0% -> 0%
where the time goes in v1:
time: 174 us
  waiting for transfers between devices  72.1 us (41%)
  Pallas kernels  59.9 us (34%)
  matrix products  20.1 us (12%)
  between operations  14.1 us (8%)
  other arithmetic  4.17 us (2%)
  local copies, waits for them, and re-layouts  3.61 us (2%)
    reduce_scatter x1, waiting for transfers between devices, on_device(): lax.psum_scatter(lax.dot_general(out_weight, normed, (((0,), (1,)), ((),...  44.5 us
    pallas_call x1, Pallas kernels, mixer(): pl.pallas_call(functools.partial(mixer_kernel, heads), grid=(sequences, g...  41 us
    all_gather x1, waiting for transfers between devices, on_device(): wide = lax.all_gather(tokens, 'head', axis=1, tiled=True).astype(F32)  26.9 us
    pallas_call x1, Pallas kernels, tail(): pl.pallas_call(functools.partial(tail_kernel, batch_count, head_count), o...  18.9 us
    dot_general x1, matrix products, on_device(): projected = jnp.dot(scaled, mix_weight, preferred_element_type=F32)  13.5 us
    dot_general x1, matrix products, on_device(): lax.dot_general(out_weight, normed, (((0,), (1,)), ((), ())), preferred_e...  4.3 us
  transfers between devices with their start and end apart: 2, of which 2 were waited for; matrix products, arithmetic and copies ran while one was open for 0% of the time, Pallas kernels for 0%

profile of v1, /device:TPU:0, one launch (start us, length us, event | category | flops | bytes accessed | tf_op | source)
XLA Modules:
  0.0 174.0 jit_solution(9049161922179857808)
XLA Ops:
  7.2 0.0 copy-start
  7.2 0.0 copy-start.4
  7.2 0.0 all-gather.2.cloned.1.call-start
  7.2 0.7 all-gather.2.cloned.1.call-update
  7.9 0.0 reduce-scatter.2.cloned.1.call-start
  8.0 26.9 %all-gather.2.cloned.1.call-done = bf16[512,2048]{1,0:T(8,128)(2,1)} async-done(((bf16[512,512]{1,0:T(8,128)(2,1)}), bf16[512,2048]{1,0:T(8,128)(2,1)}) %all-gather.2.cloned.1.call-update) | async-done | bytes 2097168 | tf_op jit(solution)/shard_map/all_gather | solution.py:405
  34.9 2.1 %fusion.1 = f32[512]{0:T(512)S(1)} fusion(bf16[512,2048]{1,0:T(8,128)(2,1)} %all-gather.2.cloned.1.call-done), kind=kLoop, calls=%fused_computation.4 | loop fusion | flops 3145216 | bytes 2099200 | tf_op jit(solution)/shard_map/reduce_sum | solution.py:407
  37.0 0.9 copy.16.inverse_ref
  37.8 2.3 %fusion.6 = f32[512,2,8]{0,2,1:T(8,128)S(1)} fusion(bf16[2048,16]{0,1:T(8,128)(2,1)} %param.17, bf16[512,2048]{1,0:T(8,128)(2,1)} %all-gather.2.cloned.1.call-done, f32[2048]{0:T(1024)} %param.15), kind=kOutput, calls=%fused_computation.8 | convolution fusion | flops 36700160 | bytes 2203648 | tf_op jit(solution)/shard_map/dot_general | solution.py:409
  40.1 1.0 copy.15
  41.1 0.0 copy-done.4
  41.1 13.5 %fusion.4.proj_ref = f32[512,3584]{1,0:T(8,128)} fusion(bf16[2048,3584]{1,0:T(8,128)(2,1)} %param.16, bf16[512,2048]{1,0:T(8,128)(2,1)} %all-gather.2.cloned.1.call-done, f32[2048]{0:T(1024)S(1)} %copy-done.4), kind=kOutput, calls=%fused_computation.7 | convolution fusion | flops 7519338496 | bytes 24125440 | tf_op jit(solution)/shard_map/dot_general | solution.py:408
  54.6 41.0 %mixer.1 = (bf16[512,512]{1,0:T(8,128)(2,1)}, f32[4,4,128,128]{3,2,1,0:T(8,128)}) custom-call(s32[4]{0:T(128)} %lengths_ref.1, f32[4]{0:T(128)} %decay_ref.1, f32[512,3584]{1,0:T(8,128)} %fusion.4.proj_ref, f32[512,1]{1,0:T(8,128)} %copy.16.inverse_ref, f32[2,512,8]{2,1,0:T(8,128)} %bitcast.25, f32[1,128]{1,0:T(1,128)} %bitcast.29, f32[4,4,128,128]{3,2,1,0:T(8,128)} %state_ref.1), custom_call_target="tpu_custom_call" | custom-call | tf_op jit(solution)/shard_map/mixer/pallas_call | solution.py:215
  95.6 0.0 copy-start.3
  95.6 0.0 copy-start.1
  95.7 4.3 %convolution_bitcast_fusion = f32[2048,512]{0,1:T(8,128)} fusion(bf16[512,512]{1,0:T(8,128)(2,1)} %get-tuple-element.5, bf16[512,2048]{1,0:T(8,128)(2,1)S(1)} %copy-done), kind=kOutput, calls=%fused_computation.5 | convolution fusion | flops 1073741824 | bytes 6815744 | tf_op jit(solution)/shard_map/dot_general | solution.py:414
  100.0 0.0 reduce-scatter.2.cloned.1.call-update
  100.1 44.5 %reduce-scatter.2.cloned.1.call-done = f32[512,512]{0,1:T(8,128)} async-done(((f32[2048,512]{0,1:T(8,128)}), f32[512,512]{0,1:T(8,128)}) %reduce-scatter.2.cloned.1.call-update) | async-done | bytes 1048592 | tf_op jit(solution)/shard_map/reduce_scatter | solution.py:413
  144.5 1.4 fusion.9
  145.9 0.0 copy-start.2
  145.9 0.6 gather_fusion
  146.5 0.7 broadcast_select_fusion.last_ref
  147.2 18.9 %tail.1 = f32[1,32]{1,0:T(1,128)} custom-call(bf16[4,512]{1,0:T(4,128)(2,1)} %broadcast_select_fusion.last_ref, f32[1,2048]{1,0:T(1,128)} %bitcast.27, bf16[512,2048]{1,0:T(8,128)(2,1)} %table_hbm.1, s32[1,32]{1,0:T(1,128)} %bitcast.30), custom_call_target="tpu_custom_call" | custom-call | tf_op jit(solution)/shard_map/tail/pallas_call | solution.py:366
  166.1 1.1 copy.18
  (10 shorter events, 0.1 us)
Async XLA Ops:
  7.2 88.5 %copy-start = (bf16[512,2048]{1,0:T(8,128)(2,1)S(1)}, bf16[512,2048]{1,0:T(8,128)(2,1)}, u32[]{:S(2)}) copy-start(bf16[512,2048]{1,0:T(8,128)(2,1)} %param.20) | copy-start | bytes 6291460
  7.2 33.9 %copy-start.4 = (f32[2048]{0:T(1024)S(1)}, f32[2048]{0:T(1024)}, u32[]{:S(2)}) copy-start(f32[2048]{0:T(1024)} %param.15) | copy-start | bytes 24580
  7.2 27.7 %all-gather.2.cloned.1.call-start = ((), (), s32[]{:S(2)}) async-start(), calls=%async_computation.1 | async-start | bytes 2621440 | tf_op jit(solution)/shard_map/all_gather | solution.py:405
  7.9 136.6 %reduce-scatter.2.cloned.1.call-start = ((), (), s32[]{:S(2)}) async-start(), calls=%async_computation.2 | async-start | bytes 5242880 | tf_op jit(solution)/shard_map/reduce_scatter | solution.py:413
  95.6 4.4 %copy-start.3 = (s32[4]{0:T(128)S(1)}, s32[4]{0:T(128)}, u32[]{:S(2)}) copy-start(s32[4]{0:T(128)} %lengths_ref.1) | copy-start | bytes 52
  95.6 48.9 %copy-start.1 = (bf16[512,512]{1,0:T(8,128)(2,1)S(1)}, bf16[512,512]{1,0:T(8,128)(2,1)}, u32[]{:S(2)}) copy-start(bf16[512,512]{1,0:T(8,128)(2,1)} %param.12) | copy-start | bytes 1572868
  145.9 21.3 %copy-start.2 = (bf16[512,512]{1,0:T(8,128)(2,1)}, bf16[512,512]{1,0:T(8,128)(2,1)S(1)}, u32[]{:S(2)}) copy-start(bf16[512,512]{1,0:T(8,128)(2,1)S(1)} %fusion.9) | copy-start | bytes 1572868
Sparse Core Ops, SparseCore 0:
  9.6 25.2 all-gather.1
  100.1 44.3 reduce-scatter.1

commit v2 on v1

--- a/solution.py
+++ b/solution.py
@@ -11,6 +11,7 @@
 NEW_POSITIONS = 128
 STEPS = NEW_POSITIONS * REFLECT
 BLOCK = 128
+PIECES = 2
 
 ROW_EPSILON = 1e-05
 KEY_EPSILON = 1e-06
@@ -233,37 +234,293 @@
             jax.ShapeDtypeStruct(states.shape, F32),
         ],
         scratch_shapes=[steps, steps, steps],
+        cost_estimate=pl.CostEstimate(
+            flops=sequences * local_heads * 2 * 10**8, bytes_accessed=2**24, transcendentals=2**22
+        ),
         name="mixer",
     )(lengths, decay_rate, projected, inverse, rates, head_gain[None], states)
 
 
-def tail_kernel(
-    batch_count,
-    head_count,
-    last_ref,
+def head_gather(own_ref, slots_ref, near_sem, far_send, far_recv, pass_send, pass_recv):
+    chips = lax.axis_size("head") // 2
+    me = lax.axis_index("head")
+    chip, core = me // 2, lax.rem(me, 2)
+    partner = 2 * chip + 1 - core
+
+    def source(shift, flip):
+        other = lax.rem(chip - shift + chips, chips)
+        return 2 * other + (1 - core if flip else core)
+
+    def near(r, slot):
+        return pltpu.make_async_remote_copy(
+            src_ref=own_ref.at[r],
+            dst_ref=slots_ref.at[slot, r],
+            send_sem=near_sem.at[0, r],
+            recv_sem=near_sem.at[1, r],
+            device_id={"head": partner},
+            device_id_type=MESH,
+        )
+
+    def far(shift, r, slot):
+        return pltpu.make_async_remote_copy(
+            src_ref=own_ref.at[r],
+            dst_ref=slots_ref.at[slot, r],
+            send_sem=far_send.at[shift, r],
+            recv_sem=far_recv.at[shift, r],
+            device_id={"head": 2 * lax.rem(chip + shift, chips) + core},
+            device_id_type=MESH,
+        )
+
+    def passed(shift, r, slot):
+        return pltpu.make_async_remote_copy(
+            src_ref=slots_ref.at[slot, r],
+            dst_ref=slots_ref.at[slot, r],
+            send_sem=pass_send.at[shift, r],
+            recv_sem=pass_recv.at[shift, r],
+            device_id={"head": partner},
+            device_id_type=MESH,
+        )
+
+    def start():
+        for r in range(PIECES):
+            for shift in range(1, chips):
+                far(shift, r, me).start()
+        for r in range(PIECES):
+            near(r, me).start()
+
+    def wait_near():
+        for r in range(PIECES):
+            near(r, partner).wait_recv()
+
+    def wait_far(r):
+        for shift in range(1, chips):
+            far(shift, r, source(shift, False)).wait_recv()
+            passed(shift, r, source(shift, False)).start()
+        for shift in range(1, chips):
+            passed(shift, r, source(shift, True)).wait_recv()
+
+    def drain():
+        for r in range(PIECES):
+            near(r, me).wait_send()
+            for shift in range(1, chips):
+                far(shift, r, me).wait_send()
+                passed(shift, r, source(shift, False)).wait_send()
+
+    order = [source(s, f) for s in range(chips) for f in (False, True)]
+    return start, wait_near, wait_far, drain, order
+
+
+def gather_scratch(head_count, rows, width):
+    chips = max(head_count // 2, 1)
+    pairs = pltpu.SemaphoreType.DMA((chips, PIECES))
+    return [
+        pltpu.VMEM((head_count, PIECES, rows // PIECES, width), BF16),
+        pltpu.SemaphoreType.DMA((2, PIECES)),
+        pairs,
+        pairs,
+        pairs,
+        pairs,
+    ]
+
+
+def project_kernel(
+    model_width,
+    own_ref,
     gain_ref,
-    table_hbm,
-    next_ref,
-    out_ref,
-    table_ref,
-    rows_ref,
-    wide_ref,
-    own_ref,
-    stats_ref,
-    table_sem,
-    row_send,
-    row_recv,
-    stat_send,
-    stat_recv,
+    rate_weight_ref,
+    mix_hbm,
+    proj_hbm,
+    inverse_ref,
+    rates_ref,
+    mix_ref,
+    scaled_ref,
+    total_ref,
+    mix_sem,
+    out_sem,
+    slots_ref,
+    *gather_sems,
 ):
+    head_count = lax.axis_size("head")
+    me = lax.axis_index("head")
+    start, wait_near, wait_far, drain, order = head_gather(own_ref, slots_ref, *gather_sems)
+    half = own_ref.shape[1]
+    rows = PIECES * half
+    tile = mix_ref.shape[2] // (2 * REFLECT + 1)
+
+    def load(slot):
+        return pltpu.make_async_copy(mix_hbm.at[slot], mix_ref.at[slot], mix_sem.at[slot])
+
+    for slot in order:
+        load(slot).start()
+    barrier = pltpu.get_barrier_semaphore()
+    for k in range(1, head_count):
+        pl.semaphore_signal(
+            barrier, inc=1, device_id={"head": lax.rem(me + k, head_count)}, device_id_type=MESH
+        )
+    pl.semaphore_wait(barrier, head_count - 1)
+    start()
+
+    def prepare(ref, slot, r):
+        wide = ref.astype(F32)
+        scaled = (wide * gain_ref[slot]).astype(BF16)
+        scaled_ref[slot, r * half : (r + 1) * half, :] = scaled
+        square = jnp.sum(wide * wide, axis=1, keepdims=True)
+        return square, jnp.dot(scaled, rate_weight_ref[slot], preferred_element_type=F32)
+
+    squares, rates = [], []
+    for r in range(PIECES):
+        square, rate = prepare(own_ref[r], order[0], r)
+        squares.append(square)
+        rates.append(rate)
+    load(order[0]).wait()
+
+    @pl.loop(0, 2 * REFLECT + 1)
+    def _(t):
+        columns = pl.ds(pl.multiple_of(t * tile, HEAD_DIM), tile)
+        total_ref[:, columns] = jnp.dot(
+            scaled_ref[order[0]], mix_ref[order[0], :, columns], preferred_element_type=F32
+        )
+
+    wait_near()
+    for r in range(PIECES):
+        square, rate = prepare(slots_ref[order[1], r], order[1], r)
+        squares[r], rates[r] = squares[r] + square, rates[r] + rate
+    load(order[1]).wait()
+
+    @pl.loop(0, 2 * REFLECT + 1)
+    def _(t):
+        columns = pl.ds(pl.multiple_of(t * tile, HEAD_DIM), tile)
+        total_ref[:, columns] += jnp.dot(
+            scaled_ref[order[1]], mix_ref[order[1], :, columns], preferred_element_type=F32
+        )
+
+    for slot in order[2:]:
+        load(slot).wait()
+    outs = []
+    for r in range(PIECES):
+        wait_far(r)
+        here = slice(r * half, (r + 1) * half)
+        for slot in order[2:]:
+            square, rate = prepare(slots_ref[slot, r], slot, r)
+            squares[r], rates[r] = squares[r] + square, rates[r] + rate
+        inverse_ref[here, :] = lax.rsqrt(squares[r] / model_width + ROW_EPSILON)
+        rates_ref[here, :] = rates[r]
+
+        @pl.loop(0, 2 * REFLECT + 1)
+        def _(t):
+            columns = pl.ds(pl.multiple_of(t * tile, HEAD_DIM), tile)
+            partial = total_ref[here, columns]
+            for slot in order[2:]:
+                partial = partial + jnp.dot(
+                    scaled_ref[slot, here, :],
+                    mix_ref[slot, :, columns],
+                    preferred_element_type=F32,
+                )
+            total_ref[here, columns] = partial
+
+        out = pltpu.make_async_copy(
+            total_ref.at[pl.ds(r * half, half)], proj_hbm.at[pl.ds(r * half, half)], out_sem.at[r]
+        )
+        out.start()
+        outs.append(out)
+    drain()
+    for out in outs:
+        out.wait()
+
+
+def project(tokens, norm_gain, mix_weight, rate_weight):
+    head_count = lax.axis_size("head")
+    rows, width = tokens.shape
+    columns, rate_columns = mix_weight.shape[1], rate_weight.shape[1]
+    vmem = pl.BlockSpec(memory_space=pltpu.VMEM)
+    hbm = pl.BlockSpec(memory_space=pl.ANY)
+    return pl.pallas_call(
+        functools.partial(project_kernel, norm_gain.shape[0]),
+        out_shape=[
+            jax.ShapeDtypeStruct((rows, columns), F32),
+            jax.ShapeDtypeStruct((rows, 1), F32),
+            jax.ShapeDtypeStruct((rows, rate_columns), F32),
+        ],
+        in_specs=[vmem, vmem, vmem, hbm],
+        out_specs=[hbm, vmem, vmem],
+        scratch_shapes=[
+            pltpu.VMEM((head_count, width, columns), BF16),
+            pltpu.VMEM((head_count, rows, width), BF16),
+            pltpu.VMEM((rows, columns), F32),
+            pltpu.SemaphoreType.DMA((head_count,)),
+            pltpu.SemaphoreType.DMA((PIECES,)),
+        ]
+        + gather_scratch(head_count, rows, width),
+        compiler_params=pltpu.CompilerParams(collective_id=2, has_side_effects=True),
+        name="project",
+    )(
+        tokens.reshape(PIECES, rows // PIECES, width),
+        norm_gain.reshape(head_count, 1, width),
+        rate_weight.reshape(head_count, width, rate_columns),
+        mix_weight.reshape(head_count, width, columns),
+    )
+
+
+def swapped_weights(out_weight, width):
+    head_count = lax.axis_size("head")
+    chips = head_count // 2
+    me = lax.axis_index("head")
+    chip, core = me // 2, lax.rem(me, 2)
+    pieces = []
+    for shift in range(chips):
+        for flip in range(2):
+            to = 2 * lax.rem(chip + shift, chips) + lax.rem(core + flip, 2)
+            piece = lax.dynamic_slice_in_dim(out_weight, to * width, width, axis=1)
+            if shift or flip:
+                route = [
+                    (2 * a + b, 2 * ((a + shift) % chips) + (b + flip) % 2)
+                    for a in range(chips)
+                    for b in range(2)
+                ]
+                piece = lax.ppermute(piece, "head", route)
+            pieces.append(piece)
+    return pieces
+
+
+def finish_kernel(batch_count, head_count, *refs):
+    lengths_ref, own_ref, tokens_ref, gain_ref, next_ref, table_hbm = refs[:6]
+    weights_hbm = refs[6 : 6 + head_count]
+    (
+        mixed_ref,
+        out_ref,
+        weight_ref,
+        sum_ref,
+        last_ref,
+        table_ref,
+        rows_ref,
+        wide_ref,
+        stat_ref,
+        stats_ref,
+        table_sem,
+        weight_sem,
+        row_send,
+        row_recv,
+        stat_send,
+        stat_recv,
+        slots_ref,
+    ) = refs[6 + head_count : 23 + head_count]
+    gather_sems = refs[23 + head_count :]
     count = batch_count * head_count
     batch_at, head_at = lax.axis_index("batch"), lax.axis_index("head")
     me = batch_at * head_count + head_at
     sequences, width = last_ref.shape
+    half = own_ref.shape[1]
     vocab_here = table_ref.shape[0]
-
-    load = pltpu.make_async_copy(table_hbm, table_ref, table_sem)
-    load.start()
+    start, wait_near, wait_far, drain, order = head_gather(own_ref, slots_ref, *gather_sems)
+
+    loads = [
+        pltpu.make_async_copy(weights_hbm[k], weight_ref.at[k], weight_sem.at[k])
+        for k in range(head_count)
+    ]
+    for load in loads:
+        load.start()
+    table_load = pltpu.make_async_copy(table_hbm, table_ref, table_sem)
+    table_load.start()
 
     def other(k):
         index = lax.rem(me + k, count)
@@ -276,6 +533,38 @@
         pl.semaphore_signal(barrier, inc=1, device_id=other(k)[1], device_id_type=MESH)
 
     pl.semaphore_wait(barrier, count - 1)
+    start()
+    for load in loads:
+        load.wait()
+    for r in range(PIECES):
+        here = slice(r * half, (r + 1) * half)
+        sum_ref[here, :] = jnp.dot(own_ref[r], weight_ref[0], preferred_element_type=F32)
+    wait_near()
+    for r in range(PIECES):
+        here = slice(r * half, (r + 1) * half)
+        sum_ref[here, :] += jnp.dot(
+            slots_ref[order[1], r], weight_ref[1], preferred_element_type=F32
+        )
+    for r in range(PIECES):
+        wait_far(r)
+        here = slice(r * half, (r + 1) * half)
+        partial = sum_ref[here, :]
+        for k in range(2, head_count):
+            partial = partial + jnp.dot(
+                slots_ref[order[k], r], weight_ref[k], preferred_element_type=F32
+            )
+        sum_ref[here, :] = tokens_ref[here, :].astype(F32) + partial
+    position = lax.broadcasted_iota(jnp.int32, (NEW_POSITIONS, width), 0)
+    for s in range(sequences):
+        here = slice(s * NEW_POSITIONS, (s + 1) * NEW_POSITIONS)
+        block = sum_ref[here, :]
+        chosen = jnp.where(position == lengths_ref[s] - 1, block, 0.0)
+        last_ref[s : s + 1, :] = (
+            jnp.sum(chosen, axis=0, keepdims=True).astype(BF16).astype(F32)
+        )
+    for r in range(PIECES):
+        here = slice(r * half, (r + 1) * half)
+        mixed_ref[here, :] = sum_ref[here, :].astype(BF16)
 
     def row_copy(k, slot):
         return pltpu.make_async_remote_copy(
@@ -292,6 +581,7 @@
         row_copy(k, me).start()
 
     rows_ref[me] = last_ref[...]
+    drain()
 
     @pl.loop(1, count)
     def _(k):
@@ -301,26 +591,26 @@
         for h in range(head_count):
             wide_ref[b * sequences : (b + 1) * sequences, h * width : (h + 1) * width] = rows_ref[
                 b * head_count + h
-            ].astype(F32)
+            ]
     everyone = wide_ref[...]
     factor = lax.rsqrt(jnp.mean(everyone * everyone, axis=1, keepdims=True) + ROW_EPSILON)
     hidden = (everyone * factor * gain_ref[...]).astype(BF16)
-    load.wait()
+    table_load.wait()
     logits = lax.dot_general(
         table_ref[...], hidden, (((1,), (1,)), ((), ())), preferred_element_type=F32
     )
     ids = lax.broadcasted_iota(jnp.int32, logits.shape, 0) + me * vocab_here
     largest = jnp.max(logits, axis=0, keepdims=True)
-    own_ref[0:1, :] = largest
-    own_ref[1:2, :] = jnp.sum(jnp.exp(logits - largest), axis=0, keepdims=True)
-    own_ref[2:3, :] = jnp.sum(
+    stat_ref[0:1, :] = largest
+    stat_ref[1:2, :] = jnp.sum(jnp.exp(logits - largest), axis=0, keepdims=True)
+    stat_ref[2:3, :] = jnp.sum(
         jnp.where(ids == next_ref[...], logits, 0.0), axis=0, keepdims=True
     )
-    own_ref[3:, :] = jnp.zeros((own_ref.shape[0] - 3, own_ref.shape[1]), F32)
+    stat_ref[3:, :] = jnp.zeros((stat_ref.shape[0] - 3, stat_ref.shape[1]), F32)
 
     def stat_copy(k, slot):
         return pltpu.make_async_remote_copy(
-            src_ref=own_ref,
+            src_ref=stat_ref,
             dst_ref=stats_ref.at[slot],
             send_sem=stat_send.at[k],
             recv_sem=stat_recv.at[slot],
@@ -332,7 +622,7 @@
     def _(k):
         stat_copy(k, me).start()
 
-    stats_ref[me] = own_ref[...]
+    stats_ref[me] = stat_ref[...]
 
     @pl.loop(1, count)
     def _(k):
@@ -356,33 +646,53 @@
         stat_copy(k, me).wait_send()
 
 
-def tail(last_rows, final_gain, vocab_table, next_token):
+def finish(normed, weights, tokens, lengths, final_gain, vocab_table, next_token):
     batch_count, head_count = lax.axis_size("batch"), lax.axis_size("head")
     count = batch_count * head_count
-    sequences, width = last_rows.shape
+    rows, width = tokens.shape
+    sequences = lengths.shape[0]
     everyone = next_token.shape[0]
     vmem = pl.BlockSpec(memory_space=pltpu.VMEM)
+    hbm = pl.BlockSpec(memory_space=pl.ANY)
     semaphores = pltpu.SemaphoreType.DMA((count,))
-    return pl.pallas_call(
-        functools.partial(tail_kernel, batch_count, head_count),
-        out_shape=jax.ShapeDtypeStruct((1, everyone), F32),
-        in_specs=[vmem, vmem, pl.BlockSpec(memory_space=pl.ANY), vmem],
-        out_specs=vmem,
+    mixed, scores = pl.pallas_call(
+        functools.partial(finish_kernel, batch_count, head_count),
+        out_shape=[
+            jax.ShapeDtypeStruct((rows, width), BF16),
+            jax.ShapeDtypeStruct((1, everyone), F32),
+        ],
+        in_specs=[pl.BlockSpec(memory_space=pltpu.SMEM), vmem, vmem, vmem, vmem, hbm]
+        + [hbm] * head_count,
+        out_specs=[vmem, vmem],
         scratch_shapes=[
+            pltpu.VMEM((head_count,) + weights[0].shape, BF16),
+            pltpu.VMEM((rows, width), F32),
+            pltpu.VMEM((sequences, width), F32),
             pltpu.VMEM(vocab_table.shape, BF16),
-            pltpu.VMEM((count, sequences, width), BF16),
+            pltpu.VMEM((count, sequences, width), F32),
             pltpu.VMEM((everyone, final_gain.shape[0]), F32),
             pltpu.VMEM((8, everyone), F32),
             pltpu.VMEM((count, 8, everyone), F32),
             pltpu.SemaphoreType.DMA,
+            pltpu.SemaphoreType.DMA((head_count,)),
             semaphores,
             semaphores,
             semaphores,
             semaphores,
-        ],
+        ]
+        + gather_scratch(head_count, rows, normed.shape[1]),
         compiler_params=pltpu.CompilerParams(collective_id=1, has_side_effects=True),
-        name="tail",
-    )(last_rows, final_gain[None], vocab_table, next_token[None])[0]
+        name="finish",
+    )(
+        lengths,
+        normed.reshape(PIECES, rows // PIECES, normed.shape[1]),
+        tokens,
+        final_gain[None],
+        next_token[None],
+        vocab_table,
+        *weights,
+    )
+    return mixed, scores[0]
 
 
 def on_device(
@@ -399,31 +709,15 @@
     vocab_table,
     next_token,
 ):
-    sequences = lengths.shape[0]
-    local_width = tokens.shape[1]
-    model_width = norm_gain.shape[0]
-    wide = lax.all_gather(tokens, "head", axis=1, tiled=True).astype(F32)
-    scaled = (wide * norm_gain).astype(BF16)
-    inverse = lax.rsqrt(jnp.sum(wide * wide, axis=1, keepdims=True) / model_width + ROW_EPSILON)
-    projected = jnp.dot(scaled, mix_weight, preferred_element_type=F32)
-    rate_logits = jnp.dot(scaled, rate_weight, preferred_element_type=F32)
+    projected, inverse, rate_logits = project(tokens, norm_gain, mix_weight, rate_weight)
+    out_weight, inverse = lax.optimization_barrier((out_weight, inverse))
+    weights = swapped_weights(out_weight, tokens.shape[1])
     normed, new_state = mixer(
         projected, inverse, rate_logits, lengths, decay_rate, head_gain, states
     )
-    mix_sum = lax.psum_scatter(
-        lax.dot_general(
-            out_weight, normed, (((0,), (1,)), ((), ())), preferred_element_type=F32
-        ),
-        "head",
-        scatter_dimension=0,
-        tiled=True,
-    ).T
-    mixed = (tokens.astype(F32) + mix_sum).astype(BF16)
-    last_index = (lengths - 1)[:, None, None]
-    last_rows = jnp.take_along_axis(
-        mixed.reshape(sequences, NEW_POSITIONS, local_width), last_index, axis=1
-    )[:, 0]
-    log_likelihood = tail(last_rows, final_gain, vocab_table, next_token)
+    mixed, log_likelihood = finish(
+        normed, weights, tokens, lengths, final_gain, vocab_table, next_token
+    )
     return (mixed, new_state, log_likelihood)
 
 

time: 174 us -> 115 us (0.66)
  waiting for transfers between devices: 72.1 us -> 0.01 us
  Pallas kernels: 59.9 us -> 104 us
  matrix products: 20.1 us -> 0 us
  between operations: 14.1 us -> 0.79 us
  local copies, waits for them, and re-layouts: 3.61 us -> 8.25 us
  other arithmetic: 4.17 us -> 0 us
  starting transfers between devices: 0.08 us -> 2.22 us
    reduce_scatter x1 -> x0, waiting for transfers between devices: 44.5 us -> none  [on_device(): lax.psum_scatter(lax.dot_general(out_weight, normed, (((0,), (1,)), ((),...]
    pallas_call x1 -> x2, Pallas kernels: 18.9 us -> 62.8 us  [the longest x1 38.6 us: finish(): pl.pallas_call(functools.partial(finish_kernel, batch_count, head_count),...]
    all_gather x1 -> x0, waiting for transfers between devices: 26.9 us -> none  [on_device(): wide = lax.all_gather(tokens, 'head', axis=1, tiled=True).astype(F32)]
    dot_general x3 -> x0, matrix products: 20.1 us -> none  [the longest x1 13.5 us: on_device(): projected = jnp.dot(scaled, mix_weight, preferred_element_type=F32)]
    unnamed x12 -> x13, local copies, waits for them, and re-layouts: 1.15 us -> 5.94 us
    ppermute x0 -> x3, starting transfers between devices: none -> 2.22 us  [swapped_weights(): piece = lax.ppermute(piece, 'head', route)]
    reduce_sum x1 -> x0, other arithmetic: 2.07 us -> none  [on_device(): jnp.sum(wide * wide, axis=1, keepdims=True) / model_width + ROW_EPSILON]
  transfers between devices with their start and end apart: 2 -> 3, of which waited for: 2 -> 0; matrix products, arithmetic and copies ran while one was open for 0% -> 1% of each run, Pallas kernels for 0% -> 36%
where the time goes in v2:
time: 115 us
  Pallas kernels  104 us (90%)
  local copies, waits for them, and re-layouts  8.25 us (7%)
  starting transfers between devices  2.22 us (2%)
    pallas_call x1, Pallas kernels, mixer(): pl.pallas_call(functools.partial(mixer_kernel, heads), grid=(sequences, g...  41 us
    pallas_call x1, Pallas kernels, finish(): pl.pallas_call(functools.partial(finish_kernel, batch_count, head_count),...  38.6 us
    pallas_call x1, Pallas kernels, project(): pl.pallas_call(functools.partial(project_kernel, norm_gain.shape[0]), out...  24.2 us
    unnamed x13, local copies, waits for them, and re-layouts  5.94 us
  transfers between devices with their start and end apart: 3, of which 0 were waited for; matrix products, arithmetic and copies ran while one was open for 1% of the time, Pallas kernels for 36%

profile of v2, /device:TPU:0, one launch (start us, length us, event | category | flops | bytes accessed | tf_op | source)
XLA Modules:
  0.0 115.1 jit_solution(932393201404390911)
XLA Ops:
  0.7 1.8 %copy.16 = bf16[2048,16]{1,0:T(8,128)(2,1)} copy(bf16[2048,16]{0,1:T(8,128)(2,1)} %param.17) | data formatting | bytes 131072 | tf_op args[5]
  2.5 24.2 %project.1 = (f32[512,3584]{1,0:T(8,128)}, f32[512,1]{1,0:T(8,128)}, f32[512,16]{1,0:T(8,128)}) custom-call(bf16[2,256,512]{2,1,0:T(8,128)(2,1)} %bitcast.12, f32[4,1,512]{2,1,0:T(1,128)} %bitcast.17, bf16[4,512,16]{2,1,0:T(8,128)(2,1)} %bitcast.13, bf16[4,512,3584]{2,1,0:T(8,128)(2,1)} %bitcast.11), custom_call_target="tpu_custom_call" | custom-call | tf_op jit(solution)/shard_map/project/pallas_call | solution.py:437
  26.7 0.0 copy-done
  26.7 0.0 copy-start.4
  26.7 1.2 %constant_dynamic-slice_fusion = (bf16[512,512]{1,0:T(8,128)(2,1)S(1)}, bf16[512,512]{1,0:T(8,128)(2,1)S(1)}, bf16[512,512]{1,0:T(8,128)(2,1)}, bf16[512,512]{1,0:T(8,128)(2,1)}) fusion(bf16[512,2048]{1,0:T(8,128)(2,1)S(1)} %copy-done, s32[]{:T(128)S(6)} %select_n.21, s32[]{:T(128)S(6)} %select_n.20, s32[]{:T(128)S(6)} %select_n.19, s32[]{:T(128)S(6)} %select_n.18), kind=kLoop, calls=%fused_computation | loop fusion | bytes 4194320 | tf_op jit(solution)/shard_map/dynamic_slice | solution.py:473
  27.9 0.6 collective-permute-start
  28.5 1.6 %collective-permute-start.1 = (bf16[512,512]{1,0:T(8,128)(2,1)S(1)}, bf16[512,512]{1,0:T(8,128)(2,1)S(1)}, u32[]{:S(2)}, u32[]{:S(2)}) collective-permute-start(bf16[512,512]{1,0:T(8,128)(2,1)S(1)} %get-tuple-element.22), channel_id=1, source_target_pairs={{0,2},{1,3},{2,0},{3,1},{4,6},{5,7},{6,4},{7,5},{8,10},{9,11},{10,... | collective-permute-start | bytes 1572872 | tf_op jit(solution)/shard_map/ppermute | solution.py:480
  30.2 0.0 collective-permute-start.2
  30.2 0.0 copy-done.4
  30.2 0.1 copy.17
  30.3 1.0 copy.18
  31.3 41.0 %mixer.1 = (bf16[512,512]{1,0:T(8,128)(2,1)}, f32[4,4,128,128]{3,2,1,0:T(8,128)}) custom-call(s32[4]{0:T(128)} %refs_0_.1, f32[4]{0:T(128)} %decay_ref.1, f32[512,3584]{1,0:T(8,128)} %get-tuple-element.12.proj_ref, f32[512,1]{1,0:T(8,128)} %get-tuple-element.14.inverse_ref, f32[2,512,8]{2,1,0:T(8,128)} %bitcast.15, f32[1,128]{1,0:T(1,128)} %bitcast.20, ...), custom_call_target="tpu_custom_call" | custom-call | flops 3200000000 | bytes 16777216 | tf_op jit(solution)/shard_map/mixer/pallas_call | solution.py:216
  72.3 0.0 collective-permute-done.refs_7_
  72.3 0.0 copy-start.1
  72.3 0.0 collective-permute-done.1.refs_8_
  72.3 0.0 copy-start.2
  72.3 0.0 collective-permute-done.2.refs_9_
  72.3 0.0 copy-start.3
  72.4 0.7 copy-done.1
  73.1 0.2 copy-done.2
  73.3 0.2 copy-done.3
  73.4 38.6 %finish.1 = (bf16[512,512]{1,0:T(8,128)(2,1)}, f32[1,32]{1,0:T(1,128)}) custom-call(s32[4]{0:T(128)} %refs_0_.1, bf16[2,256,512]{2,1,0:T(8,128)(2,1)} %bitcast.14, bf16[512,512]{1,0:T(8,128)(2,1)} %refs_2_.1, f32[1,2048]{1,0:T(1,128)} %bitcast.18, s32[1,32]{1,0:T(1,128)} %bitcast.19, bf16[512,2048]{1,0:T(8,128)(2,1)} %refs_5_.1, ...), custom_call_target="tpu_custom_call" | custom-call | tf_op jit(solution)/shard_map/finish/pallas_call | solution.py:658
  112.1 1.9 %copy.21 = bf16[512,512]{1,0:T(8,128)(2,1)} copy(bf16[512,512]{1,0:T(8,128)(2,1)} %get-tuple-element.28) | data formatting | bytes 1048576
  113.9 1.1 copy.22
  (1 shorter events, 0.0 us)
Async XLA Ops:
  2.5 24.2 %copy-start = (bf16[512,2048]{1,0:T(8,128)(2,1)S(1)}, bf16[512,2048]{1,0:T(8,128)(2,1)}, u32[]{:S(2)}) copy-start(bf16[512,2048]{1,0:T(8,128)(2,1)} %param.20) | copy-start | bytes 6291460
  26.7 3.4 %copy-start.4 = (f32[512,16]{1,0:T(8,128)S(1)}, f32[512,16]{1,0:T(8,128)}, u32[]{:S(2)}) copy-start(f32[512,16]{1,0:T(8,128)} %get-tuple-element.15) | copy-start | bytes 98308
  27.9 44.4 %collective-permute-start = (bf16[512,512]{1,0:T(8,128)(2,1)}, bf16[512,512]{1,0:T(8,128)(2,1)S(1)}, u32[]{:S(2)}, u32[]{:S(2)}) collective-permute-start(bf16[512,512]{1,0:T(8,128)(2,1)} %get-tuple-element.23), channel_id=1, source_target_pairs={{0,1},{1,0},{2,3},{3,2},{4,5},{5,4},{6,7},{7,6},{8,9},{9,8},{10,11... | collective-permute-start | bytes 1572872 | tf_op jit(solution)/shard_map/ppermute | solution.py:480
  28.5 43.8 %collective-permute-start.1 = (bf16[512,512]{1,0:T(8,128)(2,1)S(1)}, bf16[512,512]{1,0:T(8,128)(2,1)S(1)}, u32[]{:S(2)}, u32[]{:S(2)}) collective-permute-start(bf16[512,512]{1,0:T(8,128)(2,1)S(1)} %get-tuple-element.22), channel_id=1, source_target_pairs={{0,2},{1,3},{2,0},{3,1},{4,6},{5,7},{6,4},{7,5},{8,10},{9,11},{10,... | collective-permute-start | bytes 1572872 | tf_op jit(solution)/shard_map/ppermute | solution.py:480
  30.2 42.2 %collective-permute-start.2 = (bf16[512,512]{1,0:T(8,128)(2,1)S(1)}, bf16[512,512]{1,0:T(8,128)(2,1)S(1)}, u32[]{:S(2)}, u32[]{:S(2)}) collective-permute-start(bf16[512,512]{1,0:T(8,128)(2,1)S(1)} %get-tuple-element.21), channel_id=1, source_target_pairs={{0,3},{1,2},{2,1},{3,0},{4,7},{5,6},{6,5},{7,4},{8,11},{9,10},{10,... | collective-permute-start | bytes 1572872 | tf_op jit(solution)/shard_map/ppermute | solution.py:480
  72.3 0.8 copy-start.1
  72.3 0.9 copy-start.2
  72.3 1.1 copy-start.3
